TPU v7x, 32 devices: a whole 2x2x4 slice. The times are simulated.
32 devices in a mesh: rep: 1, r: 4 (over z), s: 8 (over x, y, core).
Axes of the slice: x: 2, y: 2, z: 4, core: 2. Of those that a mesh axis runs over, the one named last changes fastest.
Arguments:
- x: bfloat16 [32, 4096, 512], P(('rep', 'r', 's'))
- dy: bfloat16 [32, 4096, 512], P(('rep', 'r', 's'))
- w_gate: bfloat16 [2, 512, 3072], P(None, 's')
- w_up: bfloat16 [2, 512, 3072], P(None, 's')
- w_down: bfloat16 [2, 3072, 512], P(None, 's')
Outputs:
- output 1: bfloat16 [32, 4096, 512], P(('rep', 'r', 's'))
- output 2: bfloat16 [2, 512, 3072], P('rep', 's')
- output 3: bfloat16 [2, 512, 3072], P('rep', 's')
- output 4: bfloat16 [2, 3072, 512], P('rep', 's')
All inputs are finite; a program needn't handle non-finite values.
Results may differ from a plain program's by a relative error of at most 0.018.
Values are sent between devices in bfloat16 or wider.
A program may use at most 2 GiB of HBM per device.

v0:
```python
import jax
import jax.numpy as jnp
from jax import lax
from jax.sharding import PartitionSpec as P

NAMES = ("w_gate", "w_up", "w_down")


def matmul(a, w):
    return jnp.dot(a, w, preferred_element_type=jnp.float32).astype(jnp.bfloat16)


def normed(h):
    wide = h.astype(jnp.float32)
    scale = lax.rsqrt(jnp.mean(wide**2, -1, keepdims=True) + 1e-6)
    return (wide * scale).astype(jnp.bfloat16)


def layer(h, w):
    a = normed(h)
    gate = jnp.dot(a, w["w_gate"], preferred_element_type=jnp.float32)
    up = jnp.dot(a, w["w_up"], preferred_element_type=jnp.float32)
    return h + matmul((jax.nn.silu(gate) * up).astype(jnp.bfloat16), w["w_down"])


def solution(mesh):
    def fetched(weights, number):
        return {name: lax.all_gather(w[number], "s", axis=0, tiled=True) for name, w in zip(NAMES, weights, strict=True)}

    def summed(term):
        return lax.psum(lax.psum_scatter(term, "s", scatter_dimension=0, tiled=True), "r")

    def step(x, dy, *weights):
        layers = weights[0].shape[0]
        h, inputs = x[0], []
        for number in range(layers):
            inputs.append(h)
            h = layer(h, fetched(weights, number))
        by_h, mine = dy[0], [None] * layers
        for number in reversed(range(layers)):
            _, back = jax.vjp(lambda w, h: layer(h, w), fetched(weights, number), inputs[number])
            by_w, by_h = back(by_h)
            mine[number] = [summed(by_w[name]) for name in NAMES]
        return (by_h[None], *(jnp.stack([mine[number][i] for number in range(layers)]) for i in range(3)))

    states, cut = P(("rep", "r", "s"), None, None), P(None, "s", None)
    return jax.shard_map(
        step,
        mesh=mesh,
        in_specs=(states, states) + (cut,) * 3,
        out_specs=(states,) + (P("rep", "s", None),) * 3,
        check_vma=False,
    )
```

profile of v0, /device:TPU:0, one launch (start us, length us, event | category | flops | bytes accessed | tf_op | source)
XLA Modules:
  0.0 782.8 jit_solution(3597139149174033931)
XLA Ops:
  31.8 13.3 %all-gather.13.cloned.1.call-done = bf16[1,512,3072]{2,1,0:T(8,128)(2,1)} async-done(((bf16[1,64,3072]{2,1,0:T(8,128)(2,1)}), bf16[1,512,3072]{2,1,0:T(8,128)(2,1)}) %all-gather.13.cloned.1.call-update) | async-done | bytes 3145744 | tf_op jit(solution)/shard_map/all_gather | solution.py:28
  45.1 25.3 %fusion.47 = f32[4096,3072]{1,0:T(8,128)} fusion(bf16[1,512,3072]{2,1,0:T(8,128)(2,1)} %all-gather.13.cloned.1.call-done, bf16[1,4096,512]{1,2,0:T(8,128)(2,1)} %copy.10, f32[4096]{0:T(1024)S(1)} %fusion.57), kind=kOutput, calls=%fused_computation.75 | convolution fusion | flops 12891193344 | bytes 57688064 | tf_op jit(solution)/shard_map/dot_general | solution.py:21
  70.5 8.5 %all-gather.15.cloned.1.call-done = bf16[1,512,3072]{2,1,0:T(8,128)(2,1)} async-done(((bf16[1,64,3072]{2,1,0:T(8,128)(2,1)}), bf16[1,512,3072]{2,1,0:T(8,128)(2,1)}) %all-gather.15.cloned.1.call-update) | async-done | bytes 3145744 | tf_op jit(solution)/shard_map/all_gather | solution.py:28
  79.0 46.7 %multiply_convert_fusion.1 = (bf16[4096,3072]{1,0:T(8,128)(2,1)}, f32[4096,3072]{1,0:T(8,128)}) fusion(f32[4096,3072]{1,0:T(8,128)} %fusion.47, bf16[1,512,3072]{2,1,0:T(8,128)(2,1)} %all-gather.15.cloned.1.call-done, bf16[1,4096,512]{1,2,0:T(8,128)(2,1)} %copy.10, f32[4096]{0:T(1024)S(1)} %fusion.57), kind=kOutput, calls=%fused_computation.13 | convolution fusion | flops 12966690816 | bytes 133185536 | tf_op jit(solution)/shard_map/dot_general | solution.py:22
  125.7 21.9 %fusion.18 = (f32[4096]{0:T(1024)S(1)}, bf16[4096,512]{0,1:T(8,128)(2,1)}) fusion(bf16[4096,3072]{1,0:T(8,128)(2,1)} %get-tuple-element.20, bf16[1,3072,512]{2,1,0:T(8,128)(2,1)} %all-gather.17.cloned.1.call-done, bf16[1,4096,512]{1,2,0:T(8,128)(2,1)} %copy.10), kind=kOutput, calls=%fused_computation.40 | convolution fusion | flops 12895383552 | bytes 36716544 | tf_op jit(solution)/shard_map/dot_general | solution.py:10
  147.7 21.2 %convolution_convert_fusion.1 = bf16[4096,3072]{1,0:T(8,128)(2,1)} fusion(bf16[1,4096,512]{2,1,0:T(8,128)(2,1)} %param.6, bf16[1,3072,512]{2,1,0:T(8,128)(2,1)} %all-gather.21.cloned.1.call-done), kind=kOutput, calls=%fused_computation.22 | convolution fusion | flops 12897484800 | bytes 32505856 | tf_op jit(solution)/shard_map/transpose(jvp())/dot_general | solution.py:10
  168.8 11.9 %all-gather.23.cloned.1.call-done = bf16[1,512,3072]{2,1,0:T(8,128)(2,1)} async-done(((bf16[1,64,3072]{2,1,0:T(8,128)(2,1)}), bf16[1,512,3072]{2,1,0:T(8,128)(2,1)}) %all-gather.23.cloned.1.call-update) | async-done | bytes 3145744 | tf_op jit(solution)/shard_map/all_gather | solution.py:28
  180.7 25.5 %fusion.34 = f32[4096,3072]{1,0:T(8,128)} fusion(bf16[1,512,3072]{2,1,0:T(8,128)(2,1)} %all-gather.23.cloned.1.call-done, bf16[4096,512]{0,1:T(8,128)(2,1)} %get-tuple-element.23, f32[4096]{0:T(1024)S(1)} %fusion.58), kind=kOutput, calls=%fused_computation.62 | convolution fusion | flops 12891193344 | bytes 57688064 | tf_op jit(solution)/shard_map/jvp()/dot_general | solution.py:22
  206.2 8.8 %all-gather.19.cloned.1.call-done = bf16[1,512,3072]{2,1,0:T(8,128)(2,1)} async-done(((bf16[1,64,3072]{2,1,0:T(8,128)(2,1)}), bf16[1,512,3072]{2,1,0:T(8,128)(2,1)}) %all-gather.19.cloned.1.call-update) | async-done | bytes 3145744 | tf_op jit(solution)/shard_map/all_gather | solution.py:28
  215.0 61.1 %fusion.1 = (bf16[4096,3072]{1,0:T(8,128)(2,1)}, f32[4096,3072]{1,0:T(8,128)}) fusion(f32[4096,3072]{1,0:T(8,128)} %fusion.34, bf16[4096,3072]{1,0:T(8,128)(2,1)} %convolution_convert_fusion.1, bf16[1,512,3072]{2,1,0:T(8,128)(2,1)} %all-gather.19.cloned.1.call-done, bf16[4096,512]{0,1:T(8,128)(2,1)} %get-tuple-element.23, f32[4096]{0:T(1024)S(1)} %fusion.58), kind=kOutput, calls=%fused_computation.7 | convolution fusion | flops 13042188288 | bytes 158351360 | tf_op jit(solution)/shard_map/jvp()/dot_general | solution.py:21
  276.1 29.9 %fusion.22 = bf16[4096,512]{0,1:T(8,128)(2,1)} fusion(bf16[4096,3072]{1,0:T(8,128)(2,1)} %convolution_convert_fusion.1, bf16[1,512,3072]{2,1,0:T(8,128)(2,1)} %all-gather.23.cloned.1.call-done, f32[4096,3072]{1,0:T(8,128)} %get-tuple-element.25), kind=kOutput, calls=%fused_computation.44 | convolution fusion | flops 12962496512 | bytes 82837504 | tf_op jit(solution)/shard_map/transpose(jvp())/dot_general | solution.py:22
  306.0 22.8 %fusion.20 = (f32[4096]{0:T(1024)S(1)}, bf16[4096,512]{0,1:T(8,128)(2,1)}) fusion(bf16[4096,512]{0,1:T(8,128)(2,1)} %get-tuple-element.23, bf16[4096,512]{0,1:T(8,128)(2,1)} %fusion.22, bf16[4096,3072]{1,0:T(8,128)(2,1)} %get-tuple-element.24, bf16[1,512,3072]{2,1,0:T(8,128)(2,1)} %all-gather.19.cloned.1.call-done), kind=kOutput, calls=%fused_computation.42 | convolution fusion | flops 12895383552 | bytes 40910848 | tf_op jit(solution)/shard_map/transpose(jvp())/dot_general | solution.py:21
  335.3 20.9 %convolution_convert_fusion.7 = bf16[3072,512]{1,0:T(8,128)(2,1)} fusion(bf16[4096,3072]{1,0:T(8,128)(2,1)} %get-tuple-element.20, bf16[4096,512]{0,1:T(8,128)(2,1)} %fusion.31), kind=kOutput, calls=%fused_computation.56 | convolution fusion | flops 12886474752 | bytes 32505856 | tf_op jit(solution)/shard_map/transpose(jvp())/dot_general | solution.py:10
  356.2 35.8 %fusion.26 = bf16[3072,512]{1,0:T(8,128)(2,1)} fusion(f32[4096,3072]{1,0:T(8,128)} %fusion.34, bf16[1,4096,512]{2,1,0:T(8,128)(2,1)} %param.6, f32[4096,3072]{1,0:T(8,128)} %get-tuple-element.25), kind=kOutput, calls=%fused_computation.51 | convolution fusion | flops 12961972224 | bytes 108003328 | tf_op jit(solution)/shard_map/transpose(jvp())/dot_general | solution.py:10
  392.1 58.4 %fusion.3 = (bf16[4096,3072]{1,0:T(8,128)(2,1)}, bf16[4096,3072]{1,0:T(8,128)(2,1)}) fusion(f32[4096,3072]{1,0:T(8,128)} %fusion.47, f32[4096,3072]{1,0:T(8,128)} %get-tuple-element.21, bf16[4096,512]{0,1:T(8,128)(2,1)} %fusion.31, bf16[1,3072,512]{2,1,0:T(8,128)(2,1)} %all-gather.17.cloned.1.call-done), kind=kOutput, calls=%fused_computation.9 | convolution fusion | flops 13048479744 | bytes 158334976 | tf_op jit(solution)/shard_map/transpose(jvp())/dot_general | solution.py:10
  450.5 29.8 %fusion.27 = bf16[512,3072]{1,0:T(8,128)(2,1)} fusion(bf16[4096,3072]{1,0:T(8,128)(2,1)} %get-tuple-element.29, bf16[1,4096,512]{1,2,0:T(8,128)(2,1)} %copy.10, f32[4096]{0:T(1024)S(1)} %copy-done.7, f32[4096,3072]{1,0:T(8,128)} %fusion.47), kind=kOutput, calls=%fused_computation.52 | convolution fusion | flops 12968263680 | bytes 82853888 | tf_op jit(solution)/shard_map/transpose(jvp())/dot_general | solution.py:22
  480.4 30.4 %fusion.28 = bf16[512,3072]{1,0:T(8,128)(2,1)} fusion(bf16[4096,3072]{1,0:T(8,128)(2,1)} %convolution_convert_fusion.1, bf16[4096,512]{0,1:T(8,128)(2,1)} %get-tuple-element.23, f32[4096]{0:T(1024)S(1)} %copy-done.9, f32[4096,3072]{1,0:T(8,128)} %get-tuple-element.25), kind=kOutput, calls=%fused_computation.53 | convolution fusion | flops 12968263680 | bytes 82853888 | tf_op jit(solution)/shard_map/transpose(jvp())/dot_general | solution.py:22
  510.9 20.3 %convolution_convert_fusion.5 = bf16[512,3072]{1,0:T(8,128)(2,1)} fusion(bf16[4096,3072]{1,0:T(8,128)(2,1)} %get-tuple-element.24, bf16[4096,512]{0,1:T(8,128)(2,1)} %get-tuple-element.23, f32[4096]{0:T(1024)S(1)} %copy-done.9), kind=kOutput, calls=%fused_computation.54 | convolution fusion | flops 12891193344 | bytes 32522240 | tf_op jit(solution)/shard_map/transpose(jvp())/dot_general | solution.py:21
  531.3 20.5 %convolution_convert_fusion.6 = bf16[512,3072]{1,0:T(8,128)(2,1)} fusion(bf16[4096,3072]{1,0:T(8,128)(2,1)} %get-tuple-element.28, bf16[1,4096,512]{1,2,0:T(8,128)(2,1)} %copy.10, f32[4096]{0:T(1024)S(1)} %copy-done.7), kind=kOutput, calls=%fused_computation.55 | convolution fusion | flops 12891193344 | bytes 32522240 | tf_op jit(solution)/shard_map/transpose(jvp())/dot_general | solution.py:21
  551.8 30.0 %fusion.21 = bf16[4096,512]{0,1:T(8,128)(2,1)} fusion(bf16[4096,3072]{1,0:T(8,128)(2,1)} %get-tuple-element.29, bf16[1,512,3072]{2,1,0:T(8,128)(2,1)} %all-gather.15.cloned.1.call-done, f32[4096,3072]{1,0:T(8,128)} %fusion.47), kind=kOutput, calls=%fused_computation.43 | convolution fusion | flops 12962496512 | bytes 82837504 | tf_op jit(solution)/shard_map/transpose(jvp())/dot_general | solution.py:22
  581.9 42.8 %reduce-scatter.9.cloned.1.call-done = bf16[64,3072]{1,0:T(8,128)(2,1)} async-done(((bf16[512,3072]{1,0:T(8,128)(2,1)}), bf16[64,3072]{1,0:T(8,128)(2,1)}) %reduce-scatter.9.cloned.1.call-update) | async-done | bytes 393232 | tf_op jit(solution)/shard_map/reduce_scatter | solution.py:31
  624.7 49.1 %reduce-scatter.7.cloned.1.call-done = bf16[64,3072]{1,0:T(8,128)(2,1)} async-done(((bf16[512,3072]{1,0:T(8,128)(2,1)}), bf16[64,3072]{1,0:T(8,128)(2,1)}) %reduce-scatter.7.cloned.1.call-update) | async-done | bytes 393232 | tf_op jit(solution)/shard_map/reduce_scatter | solution.py:31
  673.9 22.9 %fusion.17 = (f32[4096]{0:T(1024)S(1)}, bf16[4096,512]{0,1:T(8,128)(2,1)}) fusion(bf16[1,4096,512]{1,2,0:T(8,128)(2,1)} %copy.10, bf16[4096,512]{0,1:T(8,128)(2,1)} %fusion.21, bf16[4096,3072]{1,0:T(8,128)(2,1)} %get-tuple-element.28, bf16[1,512,3072]{2,1,0:T(8,128)(2,1)} %all-gather.13.cloned.1.call-done), kind=kOutput, calls=%fused_computation.39 | convolution fusion | flops 12895383552 | bytes 40910848 | tf_op jit(solution)/shard_map/transpose(jvp())/dot_general | solution.py:21
  709.6 61.5 %all-reduce.3.cloned.1.call-done = (bf16[1,64,3072]{2,1,0:T(8,128)(2,1)}, bf16[1,64,3072]{2,1,0:T(8,128)(2,1)}, bf16[1,64,3072]{2,1,0:T(8,128)(2,1)}, bf16[1,64,...) async-done(((bf16[1,64,3072]{2,1,0:T(8,128)(2,1)}, bf16[1,64,3072]{2,1,0:T(8,128)(2,1)}, bf16[1,64,3072]{2,1,0:T(8,128)(2,1)}, ...) | async-done | bytes 2359312 | tf_op jit(solution)/shard_map/psum | solution.py:31
  (67 shorter events, 49.0 us)
Async XLA Ops:
  7.2 38.0 %all-gather.13.cloned.1.call-start = ((), (), s32[]{:S(2)}) async-start(), calls=%async_computation.12 | async-start | bytes 3538944 | tf_op jit(solution)/shard_map/all_gather | solution.py:28
  9.3 69.7 %all-gather.15.cloned.1.call-start = ((), (), s32[]{:S(2)}) async-start(), calls=%async_computation.13 | async-start | bytes 3538944 | tf_op jit(solution)/shard_map/all_gather | solution.py:28
  11.4 114.2 %all-gather.17.cloned.1.call-start = ((), (), s32[]{:S(2)}) async-start(), calls=%async_computation.14 | async-start | bytes 3538944 | tf_op jit(solution)/shard_map/all_gather | solution.py:28
  13.6 134.1 %all-gather.21.cloned.1.call-start = ((), (), s32[]{:S(2)}) async-start(), calls=%async_computation.16 | async-start | bytes 3538944 | tf_op jit(solution)/shard_map/all_gather | solution.py:28
  14.1 166.6 %all-gather.23.cloned.1.call-start = ((), (), s32[]{:S(2)}) async-start(), calls=%async_computation.17 | async-start | bytes 3538944 | tf_op jit(solution)/shard_map/all_gather | solution.py:28
  14.7 200.2 %all-gather.19.cloned.1.call-start = ((), (), s32[]{:S(2)}) async-start(), calls=%async_computation.15 | async-start | bytes 3538944 | tf_op jit(solution)/shard_map/all_gather | solution.py:28
  15.3 566.5 %reduce-scatter.15.cloned.1.call-start = ((), (), s32[]{:S(2)}) async-start(), calls=%async_computation.10 | async-start | bytes 3538944 | tf_op jit(solution)/shard_map/reduce_scatter | solution.py:31
  24.8 0.6 copy-start.2
  25.4 53.6 %copy-start.6 = (f32[4096]{0:T(1024)}, f32[4096]{0:T(1024)S(1)}, u32[]{:S(2)}) copy-start(f32[4096]{0:T(1024)S(1)} %fusion.57) | copy-start | bytes 49156
  147.6 21.2 %copy-start.4 = (f32[4096]{0:T(1024)}, f32[4096]{0:T(1024)S(1)}, u32[]{:S(2)}) copy-start(f32[4096]{0:T(1024)S(1)} %get-tuple-element.22) | copy-start | bytes 49156
  147.6 181.2 %copy-start.8 = (f32[4096]{0:T(1024)}, f32[4096]{0:T(1024)S(1)}, u32[]{:S(2)}) copy-start(f32[4096]{0:T(1024)S(1)} %fusion.58) | copy-start | bytes 49156
  306.0 22.8 %copy-start.5 = (f32[4096]{0:T(1024)S(1)}, f32[4096]{0:T(1024)}, u32[]{:S(2)}) copy-start(f32[4096]{0:T(1024)} %copy-done.4) | copy-start | bytes 49156
  306.0 22.8 %copy-start.1 = (bf16[1,4096,512]{1,2,0:T(8,128)(2,1)S(1)}, bf16[1,4096,512]{1,2,0:T(8,128)(2,1)}, u32[]{:S(2)}) copy-start(bf16[1,4096,512]{1,2,0:T(8,128)(2,1)} %copy.9) | copy-start | bytes 12582916
  356.1 225.7 %reduce-scatter.17.cloned.1.call-start = ((), (), s32[]{:S(2)}) async-start(), calls=%async_computation.11 | async-start | bytes 3538944 | tf_op jit(solution)/shard_map/reduce_scatter | solution.py:31
  392.1 189.8 %reduce-scatter.11.cloned.1.call-start = ((), (), s32[]{:S(2)}) async-start(), calls=%async_computation.8 | async-start | bytes 3538944 | tf_op jit(solution)/shard_map/reduce_scatter | solution.py:31
  392.1 58.4 %copy-start.7 = (f32[4096]{0:T(1024)S(1)}, f32[4096]{0:T(1024)}, u32[]{:S(2)}) copy-start(f32[4096]{0:T(1024)} %copy-done.6) | copy-start | bytes 49156
  450.5 29.9 %copy-start.9 = (f32[4096]{0:T(1024)S(1)}, f32[4096]{0:T(1024)}, u32[]{:S(2)}) copy-start(f32[4096]{0:T(1024)} %copy-done.8) | copy-start | bytes 49156
  480.4 101.5 %reduce-scatter.13.cloned.1.call-start = ((), (), s32[]{:S(2)}) async-start(), calls=%async_computation.9 | async-start | bytes 3538944 | tf_op jit(solution)/shard_map/reduce_scatter | solution.py:31
  510.9 113.8 %reduce-scatter.9.cloned.1.call-start = ((), (), s32[]{:S(2)}) async-start(), calls=%async_computation.7 | async-start | bytes 3538944 | tf_op jit(solution)/shard_map/reduce_scatter | solution.py:31
  531.2 142.6 %reduce-scatter.7.cloned.1.call-start = ((), (), s32[]{:S(2)}) async-start(), calls=%async_computation.6 | async-start | bytes 3538944 | tf_op jit(solution)/shard_map/reduce_scatter | solution.py:31
  551.8 219.4 %all-reduce.3.cloned.1.call-start = ((), (), s32[]{:S(2)}) async-start(), calls=%async_computation.18 | async-start | bytes 4718592 | tf_op jit(solution)/shard_map/psum | solution.py:31
  673.9 22.9 %copy-start.3 = (f32[4096]{0:T(1024)S(1)}, f32[4096]{0:T(1024)}, u32[]{:S(2)}) copy-start(f32[4096]{0:T(1024)} %copy-done.2) | copy-start | bytes 49156
  673.9 22.9 %copy-start = (bf16[1,4096,512]{1,2,0:T(8,128)(2,1)S(1)}, bf16[1,4096,512]{1,2,0:T(8,128)(2,1)}, u32[]{:S(2)}) copy-start(bf16[1,4096,512]{1,2,0:T(8,128)(2,1)} %copy.10) | copy-start | bytes 12582916
Sparse Core Ops, SparseCore 0:
  10.4 34.6 all-gather.12
  47.0 31.8 all-gather.14
  80.9 31.8 all-gather.16
  114.5 31.8 all-gather.20
  148.8 31.8 all-gather.22
  183.0 31.8 all-gather.18
  356.3 45.8 reduce-scatter.14
  405.5 45.8 reduce-scatter.16
  480.5 45.8 reduce-scatter.10
  529.6 45.8 reduce-scatter.12
  578.9 45.8 reduce-scatter.8
  628.0 45.8 reduce-scatter.6
  676.6 94.4 all-reduce.2
where the time goes:
time: 790 us; the launch traced here: 783 us
  matrix products  523 us (66%)
  waiting for transfers between devices  198 us (25%)
  local copies, waits for them, and re-layouts  26 us (3%)
  other arithmetic  20.7 us (3%)
  between operations  14.5 us (2%)
    dot_general x6, matrix products, layer(): up = jnp.dot(a, w['w_up'], preferred_element_type=jnp.float32)  192 us
    dot_general x6, matrix products, layer(): gate = jnp.dot(a, w['w_gate'], preferred_element_type=jnp.float32)  173 us
    dot_general x5, matrix products, matmul(): jnp.dot(a, w, preferred_element_type=jnp.float32).astype(jnp.bfloat16)  158 us
    reduce_scatter x6, waiting for transfers between devices, summed(): lax.psum_scatter(term, 's', scatter_dimension=0, tiled=True)  92 us
    psum x1, waiting for transfers between devices, summed(): lax.psum(lax.psum_scatter(term, 's', scatter_dimension=0, tiled=True), 'r')  61.5 us
    all_gather x6, waiting for transfers between devices, fetched(): lax.all_gather(w[number], 's', axis=0, tiled=True)  42.5 us
    unnamed x23, local copies, waits for them, and re-layouts  19.8 us
  transfers between devices with their start and end apart: 13, of which 7 were waited for; matrix products, arithmetic and copies ran while one was open for 54% of the time, Pallas kernels for 0%

commit v1 on v0

v1 whole, which is shorter than its diff:
```python
import functools

import jax
import jax.numpy as jnp
from jax import lax
from jax.experimental import pallas as pl
from jax.experimental.pallas import tpu as pltpu
from jax.sharding import PartitionSpec as P

MESH = pl.DeviceIdType.MESH
f32, bf16 = jnp.float32, jnp.bfloat16
D, FF, F, NC, LAYERS, S, Z = 512, 3072, 512, 6, 2, 8, 4
LEAD = 3
NM = NC * LAYERS


def nn(a, b):
    return jnp.dot(a, b, preferred_element_type=f32)


def nt(a, b):
    return lax.dot_general(a, b, (((1,), (1,)), ((), ())), preferred_element_type=f32)


def normed(h):
    wide = h.astype(f32)
    return (wide * lax.rsqrt(jnp.mean(wide * wide, -1, keepdims=True) + 1e-6)).astype(bf16)


def through_norm(by_a, h):
    wide = h.astype(f32)
    scale = lax.rsqrt(jnp.mean(wide * wide, -1, keepdims=True) + 1e-6)
    along = jnp.mean(by_a * wide, -1, keepdims=True)
    return by_a * scale - wide * (scale * scale * scale * along)


def wait_for(ref, sem):
    pltpu.make_async_copy(ref, ref, sem).wait()


def kernel(T02, T1, TB, x_h, dy_h, wg_h, wu_h, wd_h,
           dx_h, ogu_h, od_h, wgu_f, wd_f, gsave, a0t_h,
           A, AT, DY, DYT, HB, ACC, WB, DW, GST, SGU,
           S1GU, S1D, R1GU, R1D, S2GU, S2D, P2GU, P2D, R2GU, R2D,
           S3GU, S3D, P3GU, P3D, R3GU, R3D, S4GU, S4D,
           st_sem, io_sem, wl_sem, g_sem, gi, di, gd, dd, ags, ads, rs):
    N = A.shape[0]
    s, z = lax.axis_index("s"), lax.axis_index("r")
    e, q = lax.rem(s, 2), lax.div(s, 2)
    qx, qy = lax.div(q, 2), lax.rem(q, 2)
    others = (2 * (1 - qx) + qy, 2 * qx + 1 - qy, 2 * (1 - qx) + 1 - qy)
    partner = {"s": 2 * q + 1 - e}

    def chip(i):
        return {"s": 2 * others[i] + e}

    def plane(i):
        return lax.rem(z + i, Z)

    def remote(src, dst, send, recv, to):
        pltpu.make_async_remote_copy(src_ref=src, dst_ref=dst, send_sem=send, recv_sem=recv, device_id=to, device_id_type=MESH).start()

    def split(kk):
        l = lax.div(kk, NC)
        c = lax.rem(kk, NC)
        return l, c, lax.rem(c, 2), lax.div(c, 2)

    def send_own(kk):
        l, c, h, j = split(kk)
        rows = pl.ds(pl.multiple_of(64 * s, 64), 64)
        src, dst = SGU.at[l, c], wgu_f.at[l, c, :, rows, :]
        for i in range(3):
            remote(src, dst, ags.at[kk], gi.at[kk], chip(i))
        remote(src, dst, ags.at[kk], gd.at[kk], partner)
        pltpu.make_async_copy(src, dst, gi.at[kk]).start()

        @pl.when(h == e)
        def _():
            src = wd_h.at[l, pl.ds(pl.multiple_of(128 * j, 128), 128), :]
            dst = wd_f.at[l, c, pl.ds(pl.multiple_of(128 * q, 128), 128), :]
            for i in range(3):
                remote(src, dst, ads.at[kk], di.at[kk], chip(i))
            remote(src, dst, ads.at[kk], dd.at[kk], partner)
            pltpu.make_async_copy(src, dst, di.at[kk]).start()

    def forward(kk):
        l, c, h, j = split(kk)
        wait_for(wgu_f.at[l, c, :, pl.ds(0, 256), :], gi.at[kk])
        for i in range(3):
            block = wgu_f.at[l, c, :, pl.ds(pl.multiple_of(64 * (2 * others[i] + e), 64), 64), :]
            remote(block, block, ags.at[kk], gd.at[kk], partner)

        @pl.when(h == e)
        def _():
            wait_for(wd_f.at[l, c], di.at[kk])
            for i in range(3):
                block = wd_f.at[l, c, pl.ds(pl.multiple_of(128 * others[i], 128), 128), :]
                remote(block, block, ads.at[kk], dd.at[kk], partner)

    def arrive(kk):
        l, c, h, j = split(kk)
        wait_for(wgu_f.at[l, c, :, pl.ds(0, 256), :], gd.at[kk])

        @pl.when(h != e)
        def _():
            wait_for(wd_f.at[l, c], dd.at[kk])

    def load(kk):
        l = lax.rem(lax.div(kk, NC), LAYERS)
        c, slot = lax.rem(kk, NC), lax.rem(kk, 2)
        pltpu.make_async_copy(wgu_f.at[l, c], WB.at[slot, pl.ds(0, 2)], wl_sem.at[slot]).start()
        pltpu.make_async_copy(wd_f.at[l, c], WB.at[slot, 2], wl_sem.at[slot]).start()

    def loaded(kk):
        slot = lax.rem(kk, 2)
        wait_for(WB.at[slot], wl_sem.at[slot])

    def sent_all(kk):
        l, c, h, j = split(kk)
        wait_for(wgu_f.at[l, c, :, pl.ds(0, 448), :], ags.at[kk])

        @pl.when(h == e)
        def _():
            wait_for(wgu_f.at[l, c, :, pl.ds(0, 448), :], ads.at[kk])

    def place(m):
        l = 1 - lax.div(m, NC)
        c = lax.rem(m, NC)
        return l, c, lax.rem(c, 2), lax.div(c, 2), lax.rem(m, 2)

    def rows64(block):
        return pl.ds(pl.multiple_of(64 * block, 64), 64)

    def pair_send(m):
        l, c, h, j, sl = place(m)

        @pl.when(m >= 1)
        def _():
            wait_for(S1GU, rs.at[0, m - 1])
        for p in range(4):
            for n in range(2):
                S1GU[p, n] = DW[sl, n, rows64(2 * p + 1 - e), :].astype(bf16)
        remote(S1GU, R1GU.at[sl], rs.at[0, m], rs.at[1, m], partner)

        @pl.when(h != e)
        def _():
            @pl.when(m >= 2)
            def _():
                wait_for(S1D, rs.at[2, m - 2])
            for p in range(4):
                S1D[p] = DW[sl, 2, :, 128 * p:128 * p + 128].astype(bf16)
            remote(S1D, R1D, rs.at[2, m], rs.at[3, m], partner)

    def pair_sum(m):
        l, c, h, j, sl = place(m)
        wait_for(R1GU.at[sl], rs.at[1, m])

        @pl.when(m >= 1)
        def _():
            wait_for(R2GU.at[0], rs.at[4, m - 1])
        for p in range(4):
            for n in range(2):
                S2GU[p, n] = (DW[sl, n, rows64(2 * p + e), :] + R1GU[sl, p, n].astype(f32)).astype(bf16)
        for n in range(2):
            P2GU[n] = DW[sl, n, rows64(2 * q + e), :] + R1GU[sl, q, n].astype(f32)
        for i in range(3):
            remote(S2GU.at[others[i]], R2GU.at[sl, i], rs.at[4, m], rs.at[5, m], chip(i))

        @pl.when(h == e)
        def _():
            wait_for(R1D, rs.at[3, m])

            @pl.when(m >= 2)
            def _():
                wait_for(R2D, rs.at[6, m - 2])
            for p in range(4):
                total = DW[sl, 2, :, 128 * p:128 * p + 128] + R1D[p].astype(f32)
                S2D[p] = total.astype(bf16)

                @pl.when(q == p)
                def _():
                    P2D[...] = total
            for i in range(3):
                remote(S2D.at[others[i]], R2D.at[i], rs.at[6, m], rs.at[7, m], chip(i))

    def plane_sum(m):
        l, c, h, j, sl = place(m)
        wait_for(R2GU.at[sl], rs.at[5, m])

        @pl.when(m >= 1)
        def _():
            wait_for(R3GU.at[0], rs.at[8, m - 1])
        for p in range(4):
            k = slice(16 * p, 16 * p + 16)
            total = P2GU[:, k, :]
            for i in range(3):
                total += R2GU[sl, i, :, k, :].astype(f32)
            S3GU[p] = total.astype(bf16)

            @pl.when(z == p)
            def _():
                P3GU[...] = total
        for i in range(1, 4):
            remote(S3GU.at[plane(i)], R3GU.at[sl, i - 1], rs.at[8, m], rs.at[9, m], {"r": plane(i)})

        @pl.when(h == e)
        def _():
            wait_for(R2D, rs.at[7, m])

            @pl.when(m >= 2)
            def _():
                wait_for(R3D, rs.at[10, m - 2])
            for p in range(4):
                k = slice(128 * p, 128 * p + 128)
                total = P2D[k, :]
                for i in range(3):
                    total += R2D[i, k, :].astype(f32)
                S3D[p] = total.astype(bf16)

                @pl.when(z == p)
                def _():
                    P3D[...] = total
            for i in range(1, 4):
                remote(S3D.at[plane(i)], R3D.at[i - 1], rs.at[10, m], rs.at[11, m], {"r": plane(i)})

    def last_sum(m):
        l, c, h, j, sl = place(m)
        wait_for(R3GU.at[sl], rs.at[9, m])

        @pl.when(m >= 1)
        def _():
            wait_for(S3GU, rs.at[12, m - 1])
        S4GU[...] = (P3GU[...] + R3GU[sl, 0].astype(f32) + R3GU[sl, 1].astype(f32) + R3GU[sl, 2].astype(f32)).astype(bf16)
        dst = ogu_h.at[l, c, z]
        for i in range(1, 4):
            remote(S4GU, dst, rs.at[12, m], rs.at[13, m], {"r": plane(i)})
        pltpu.make_async_copy(S4GU, dst, rs.at[12, m]).start()

        @pl.when(h == e)
        def _():
            wait_for(R3D, rs.at[11, m])

            @pl.when(m >= 2)
            def _():
                wait_for(S3D, rs.at[14, m - 2])
            S4D[...] = (P3D[...] + R3D[0].astype(f32) + R3D[1].astype(f32) + R3D[2].astype(f32)).astype(bf16)
            dst = od_h.at[l, j, z]
            for i in range(1, 4):
                remote(S4D, dst, rs.at[14, m], rs.at[15, m], {"r": plane(i)})
            pltpu.make_async_copy(S4D, dst, rs.at[14, m]).start()

    def ended(m):
        l, c, h, j, sl = place(m)
        wait_for(R3GU.at[0], rs.at[13, m])

        @pl.when(h == e)
        def _():
            wait_for(R3D, rs.at[15, m])

    def hooks(kk, t, NT, gathers, reduces):
        at = [NT * i // 4 for i in range(4)]

        @pl.when(t == at[0])
        def _():
            loaded(kk)
            if reduces:
                @pl.when(kk >= NC + 2)
                def _():
                    plane_sum(kk - NC - 2)

                @pl.when(kk >= NC + 1)
                def _():
                    pair_send(kk - NC - 1)

        @pl.when(t == at[1])
        def _():
            if gathers:
                @pl.when(kk + 1 < NM)
                def _():
                    forward(kk + 1)

                @pl.when(kk + LEAD < NM)
                def _():
                    send_own(kk + LEAD)
            if reduces:
                @pl.when(kk >= NC + 1)
                def _():
                    pair_sum(kk - NC - 1)

        if reduces:
            @pl.when(t == at[2])
            def _():
                @pl.when(kk >= NC + 2)
                def _():
                    last_sum(kk - NC - 2)

        @pl.when(t == at[3])
        def _():
            if gathers:
                @pl.when(kk + 1 < NM)
                def _():
                    arrive(kk + 1)

            @pl.when(kk + 1 < 3 * NC)
            def _():
                load(kk + 1)

    def tile(t, T):
        return pl.ds(pl.multiple_of(t * T, T), T)

    xin = pltpu.make_async_copy(x_h, HB, io_sem.at[0])
    dyin = pltpu.make_async_copy(dy_h, DY, io_sem.at[1])
    for l in range(LAYERS):
        def stage(c, _):
            h, j = lax.rem(c, 2), lax.div(c, 2)
            for p in range(4):
                cols = pl.ds(pl.multiple_of(384 * (2 * p + h) + 128 * j, 128), 128)
                for n, w in enumerate((wg_h, wu_h)):
                    pltpu.make_async_copy(w.at[l, :, cols], SGU.at[l, c, n, :, pl.ds(128 * p, 128)], st_sem.at[l]).start()
            return 0
        lax.fori_loop(0, NC, stage, 0)
    xin.start()
    dyin.start()
    barrier = pltpu.get_barrier_semaphore()
    peers = [partner] + [chip(i) for i in range(3)] + [{"r": plane(i)} for i in range(1, 4)]
    for to in peers:
        pl.semaphore_signal(barrier, 1, device_id=to, device_id_type=MESH)
    wait_for(SGU.at[0], st_sem.at[0])
    wait_for(SGU.at[1], st_sem.at[1])
    pl.semaphore_wait(barrier, len(peers))
    for kk in range(LEAD):
        send_own(jnp.int32(kk))
    xin.wait()
    dyin.wait()

    def prepare(t, _):
        r = tile(t, TB)
        a = normed(HB[r, :])
        A[r, :] = a
        AT[:, r] = a.T
        DYT[:, r] = DY[r, :].T
        ACC[r, :] = jnp.zeros((TB, D), f32)
        return 0

    lax.fori_loop(0, N // TB, prepare, 0)
    keep = pltpu.make_async_copy(AT, a0t_h, io_sem.at[2])
    keep.start()
    forward(jnp.int32(0))
    arrive(jnp.int32(0))
    load(jnp.int32(0))

    NT = N // T02

    def save(i, go):
        sl = lax.rem(i, 2)
        c, t = lax.div(i, NT), lax.rem(i, NT)
        cp = pltpu.make_async_copy(GST.at[sl], gsave.at[c, :, tile(t, T02), :], g_sem.at[sl])
        cp.start() if go else cp.wait()

    def phase0(i, _):
        kk, t, sl = lax.div(i, NT), lax.rem(i, NT), lax.rem(i, 2)
        hooks(kk, t, NT, True, False)

        @pl.when(i >= 2)
        def _():
            save(i - 2, False)
        w, r = lax.rem(kk, 2), tile(t, T02)
        a = A[r, :]
        g, u = nn(a, WB[w, 0]), nn(a, WB[w, 1])
        GST[sl, 0] = g
        GST[sl, 1] = u
        p = (g / (1.0 + jnp.exp(-g)) * u).astype(bf16)
        ACC[r, :] += nn(p, WB[w, 2])
        save(i, True)
        return 0

    lax.fori_loop(0, NC * NT, phase0, 0)
    save(jnp.int32(NC * NT - 2), False)
    save(jnp.int32(NC * NT - 1), False)
    keep.wait()

    def between(t, _):
        r = tile(t, TB)
        h = (HB[r, :].astype(f32) + ACC[r, :].astype(bf16).astype(f32)).astype(bf16)
        HB[r, :] = h
        a = normed(h)
        A[r, :] = a
        AT[:, r] = a.T
        ACC[r, :] = jnp.zeros((TB, D), f32)
        return 0

    lax.fori_loop(0, N // TB, between, 0)

    def backward(kk, t, T, g, u):
        w, r, sl = lax.rem(kk, 2), tile(t, T), lax.rem(kk + 1, 2)
        sl = lax.rem(kk, 2)
        by_p = nt(DY[r, :], WB[w, 2]).astype(bf16).astype(f32)
        sig = 1.0 / (1.0 + jnp.exp(-g))
        act = g * sig
        p = (act * u).astype(bf16)
        by_u = (by_p * act).astype(bf16)
        by_g = (by_p * u * (sig + act * (1.0 - sig))).astype(bf16)
        ACC[r, :] += nt(by_g, WB[w, 0]) + nt(by_u, WB[w, 1])
        first = t == 0
        DW[sl, 0] = jnp.where(first, 0.0, DW[sl, 0]) + nn(AT[:, r], by_g)
        DW[sl, 1] = jnp.where(first, 0.0, DW[sl, 1]) + nn(AT[:, r], by_u)
        DW[sl, 2] = jnp.where(first, 0.0, DW[sl, 2]) + nn(DYT[:, r], p)

    NT1 = N // T1

    def phase1(i, _):
        kk, t = NC + lax.div(i, NT1), lax.rem(i, NT1)
        hooks(kk, t, NT1, True, True)
        w, a = lax.rem(kk, 2), A[tile(t, T1), :]
        backward(kk, t, T1, nn(a, WB[w, 0]), nn(a, WB[w, 1]))
        return 0

    lax.fori_loop(0, NC * NT1, phase1, 0)
    again = pltpu.make_async_copy(a0t_h, AT, io_sem.at[2])
    again.start()

    def fetch(i, go):
        sl = lax.rem(i, 2)
        c, t = lax.div(i, NT), lax.rem(i, NT)
        cp = pltpu.make_async_copy(gsave.at[c, :, tile(t, T02), :], GST.at[sl], g_sem.at[sl])
        cp.start() if go else cp.wait()

    fetch(jnp.int32(0), True)

    def turn(t, _):
        r = tile(t, TB)
        by_a = ACC[r, :].astype(bf16).astype(f32)
        by_h = (DY[r, :].astype(f32) + through_norm(by_a, HB[r, :]).astype(bf16).astype(f32)).astype(bf16)
        DY[r, :] = by_h
        DYT[:, r] = by_h.T
        ACC[r, :] = jnp.zeros((TB, D), f32)
        return 0

    lax.fori_loop(0, N // TB, turn, 0)
    xin.start()
    again.wait()

    def phase2(i, _):
        kk, t, sl = 2 * NC + lax.div(i, NT), lax.rem(i, NT), lax.rem(i, 2)
        hooks(kk, t, NT, False, True)

        @pl.when(i + 1 < NC * NT)
        def _():
            fetch(i + 1, True)
        fetch(i, False)
        backward(kk, t, T02, GST[sl, 0], GST[sl, 1])
        return 0

    lax.fori_loop(0, NC * NT, phase2, 0)
    plane_sum(jnp.int32(NM - 2))
    pair_send(jnp.int32(NM - 1))
    xin.wait()

    def out(t):
        return pltpu.make_async_copy(DY.at[tile(t, TB)], dx_h.at[tile(t, TB)], io_sem.at[1])

    def finish(t, _):
        r = tile(t, TB)
        by_a = ACC[r, :].astype(bf16).astype(f32)
        DY[r, :] = (DY[r, :].astype(f32) + through_norm(by_a, HB[r, :]).astype(bf16).astype(f32)).astype(bf16)
        return 0

    half = N // TB // 2
    lax.fori_loop(0, half, finish, 0)
    pair_sum(jnp.int32(NM - 1))
    last_sum(jnp.int32(NM - 2))
    lax.fori_loop(half, N // TB, finish, 0)
    dxout = pltpu.make_async_copy(DY, dx_h, io_sem.at[1])
    dxout.start()
    plane_sum(jnp.int32(NM - 1))
    last_sum(jnp.int32(NM - 1))

    def settle(kk, _):
        sent_all(kk)
        ended(kk)
        return 0

    lax.fori_loop(0, NM, settle, 0)
    wait_for(S1GU, rs.at[0, NM - 1])
    wait_for(R2GU.at[0], rs.at[4, NM - 1])
    wait_for(R3GU.at[0], rs.at[8, NM - 1])
    wait_for(S3GU, rs.at[12, NM - 1])

    def last_d(m):
        wait_for(R2D, rs.at[6, m])
        wait_for(R3D, rs.at[10, m])
        wait_for(S3D, rs.at[14, m])

    @pl.when(e == 0)
    def _():
        wait_for(S1D, rs.at[2, NM - 1])
        last_d(NM - 2)

    @pl.when(e == 1)
    def _():
        wait_for(S1D, rs.at[2, NM - 2])
        last_d(NM - 1)
    dxout.wait()


def solution(mesh, T02=512, T1=1024, TB=512):
    def step(x, dy, w_gate, w_up, w_down):
        N = x.shape[1]
        hbm = pl.BlockSpec(memory_space=pl.ANY)
        sds = jax.ShapeDtypeStruct
        v, dma = pltpu.VMEM, pltpu.SemaphoreType.DMA
        dx, ogu, od, *_ = pl.pallas_call(
            functools.partial(kernel, min(T02, N), min(T1, N), min(TB, N)),
            name="step",
            out_shape=[
                sds((N, D), bf16), sds((LAYERS, NC, Z, 2, 16, F), bf16), sds((LAYERS, 3, Z, 128, 128), bf16),
                sds((LAYERS, NC, 2, D, F), bf16), sds((LAYERS, NC, F, D), bf16), sds((NC, 2, N, F), f32), sds((D, N), bf16),
            ],
            in_specs=[hbm] * 5,
            out_specs=[hbm] * 7,
            scratch_shapes=[
                v((N, D), bf16), v((D, N), bf16), v((N, D), bf16), v((D, N), bf16), v((N, D), bf16), v((N, D), f32),
                v((2, 3, 512, 512), bf16), v((2, 3, 512, 512), f32), v((2, 2, min(T02, N), F), f32), v((LAYERS, NC, 2, 64, F), bf16),
                v((4, 2, 64, F), bf16), v((4, D, 128), bf16), v((2, 4, 2, 64, F), bf16), v((4, D, 128), bf16),
                v((4, 2, 64, F), bf16), v((4, D, 128), bf16), v((2, 64, F), f32), v((D, 128), f32), v((2, 3, 2, 64, F), bf16), v((3, D, 128), bf16),
                v((4, 2, 16, F), bf16), v((4, 128, 128), bf16), v((2, 16, F), f32), v((128, 128), f32), v((2, 3, 2, 16, F), bf16), v((3, 128, 128), bf16),
                v((2, 16, F), bf16), v((128, 128), bf16),
                dma((2,)), dma((3,)), dma((2,)), dma((2,)), dma((NM,)), dma((NM,)), dma((NM,)), dma((NM,)), dma((NM,)), dma((NM,)), dma((16, NM)),
            ],
            compiler_params=pltpu.CompilerParams(collective_id=0, has_side_effects=True, vmem_limit_bytes=67043328),
        )(x[0], dy[0], w_gate, w_up, w_down)
        gu = ogu.reshape(LAYERS, 3, 2, Z, 2, 16, 4, 128).transpose(4, 0, 3, 5, 6, 2, 1, 7).reshape(2, LAYERS, 64, FF)
        down = od.transpose(0, 1, 4, 2, 3).reshape(LAYERS, 384, D)
        return dx[None], gu[0], gu[1], down

    states, cut = P(("rep", "r", "s"), None, None), P(None, "s", None)
    return jax.shard_map(
        step,
        mesh=mesh,
        in_specs=(states, states) + (cut,) * 3,
        out_specs=(states,) + (P("rep", "s", None),) * 3,
        check_vma=False,
    )
```

time: 790 us -> 344 us (0.44)
  matrix products: 523 us -> 0 us
  Pallas kernels: 0 us -> 329 us
  waiting for transfers between devices: 198 us -> 0 us
  other arithmetic: 20.7 us -> 0 us
  between operations: 14.5 us -> 0.68 us
  local copies, waits for them, and re-layouts: 26 us -> 13.5 us
    dot_general x17 -> x0, matrix products: 523 us -> none  [the longest x6 192 us: layer(): up = jnp.dot(a, w['w_up'], preferred_element_type=jnp.float32)]
    pallas_call x0 -> x1, Pallas kernels: none -> 329 us  [step(): pl.pallas_call(functools.partial(kernel, min(T02, N), min(T1, N), min(TB,...]
    reduce_scatter x6 -> x0, waiting for transfers between devices: 92 us -> none  [summed(): lax.psum_scatter(term, 's', scatter_dimension=0, tiled=True)]
    psum x1 -> x0, waiting for transfers between devices: 61.5 us -> none  [summed(): lax.psum(lax.psum_scatter(term, 's', scatter_dimension=0, tiled=True), 'r')]
    all_gather x6 -> x0, waiting for transfers between devices: 42.5 us -> none  [fetched(): lax.all_gather(w[number], 's', axis=0, tiled=True)]
    unnamed x23 -> x3, local copies, waits for them, and re-layouts: 19.8 us -> 4.47 us
  transfers between devices with their start and end apart: 13 -> 0, of which waited for: 7 -> 0; matrix products, arithmetic and copies ran while one was open for 54% -> 0% of each run, Pallas kernels for 0% -> 0%
where the time goes in v1:
time: 344 us
  Pallas kernels  329 us (96%)
  local copies, waits for them, and re-layouts  13.5 us (4%)
    pallas_call x1, Pallas kernels, step(): pl.pallas_call(functools.partial(kernel, min(T02, N), min(T1, N), min(TB,...  329 us

profile of v1, /device:TPU:0, one launch (start us, length us, event | category | flops | bytes accessed | tf_op | source)
XLA Modules:
  0.0 343.7 jit_solution(4380946881070511288)
XLA Ops:
  0.6 329.5 %step.1 = (bf16[4096,512]{1,0:T(8,128)(2,1)}, bf16[2,6,4,2,16,512]{5,4,3,2,1,0:T(8,128)(2,1)}, bf16[2,3,4,128,128]{4,3,2,1,0:T(8,128)(2,1)}, bf16[2,6,2,512,512]...) custom-call(bf16[4096,512]{1,0:T(8,128)(2,1)} %bitcast.11, ...), custom_call_target="tpu_custom_call" | custom-call | tf_op jit(solution)/shard_map/step/pallas_call | solution.py:512
  330.1 0.0 copy-start
  330.1 1.6 copy.12
  331.8 1.2 reshape.20
  333.0 0.0 copy-done
  333.0 0.4 reshape.19
  333.4 2.2 copy.14
  335.5 0.8 fusion
  336.3 1.4 squeeze.15
  337.8 1.4 squeeze.14
  339.2 4.5 %copy.16 = bf16[1,4096,512]{2,1,0:T(8,128)(2,1)} copy(bf16[1,4096,512]{2,1,0:T(8,128)(2,1)} %bitcast.10) | data formatting | bytes 8388608
Async XLA Ops:
  330.1 2.8 copy-start

commit v2 on v1

v2 whole, which is shorter than its diff:
```python
import functools

import jax
import jax.numpy as jnp
from jax import lax
from jax.experimental import pallas as pl
from jax.experimental.pallas import tpu as pltpu
from jax.sharding import PartitionSpec as P

MESH = pl.DeviceIdType.MESH
DOWN = 2
LANES, ROWS, QUARTER = 128, 64, 16
PAIR_OUT, PAIR_IN, PLANE_OUT, PLANE_IN, ACROSS_OUT, ACROSS_IN, ROUND_OUT, ROUND_IN = range(8)
f32, bf16 = jnp.float32, jnp.bfloat16
D, FF, F, NC, LAYERS, S, Z = 512, 3072, 512, 6, 2, 8, 4
SUB = 512
NM = NC * LAYERS


def odd(n):
    return lax.rem(n, 2)


def nn(a, b):
    return jnp.dot(a, b, preferred_element_type=f32)


def nt(a, b):
    return lax.dot_general(a, b, (((1,), (1,)), ((), ())), preferred_element_type=f32)


def normed(h):
    wide = h.astype(f32)
    return (wide * lax.rsqrt(jnp.mean(wide * wide, -1, keepdims=True) + 1e-6)).astype(bf16)


def through_norm(by_a, h):
    wide = h.astype(f32)
    scale = lax.rsqrt(jnp.mean(wide * wide, -1, keepdims=True) + 1e-6)
    along = jnp.mean(by_a * wide, -1, keepdims=True)
    return by_a * scale - wide * (scale * scale * scale * along)


def wait_for(ref, sem):
    pltpu.make_async_copy(ref, ref, sem).wait()


def kernel(T, TB, x_h, dy_h, wg_h, wu_h, wd_h,
           dx_h, ogu_h, od_h, wgu_f, wd_f, gsave_h, a0t_h,
           A, AT, DY, DYT, HB, ACC, WB, DW, GST, SGU,
           S1GU, S1D, R1GU, R1D, S2GU, S2D, P2GU, P2D, R2GU, R2D,
           S3GU, S3D, P3GU, P3D, R3GU, R3D, S4GU, S4D,
           st_sem, io_sem, wl_sem, g_sem, gi, di, dz, gd, dd, ags, ads, x_sem, rs):
    N = A.shape[0]
    s, z = lax.axis_index("s"), lax.axis_index("r")
    e, q = odd(s), lax.div(s, 2)
    qx, qy = lax.div(q, 2), odd(q)
    others = (2 * (1 - qx) + qy, 2 * qx + 1 - qy, 2 * (1 - qx) + 1 - qy)
    partner = {"s": 2 * q + 1 - e}

    def chip(i):
        return {"s": 2 * others[i] + e}

    def plane(i):
        return lax.rem(z + i, Z)

    def remote(src, dst, send, recv, to):
        pltpu.make_async_remote_copy(src_ref=src, dst_ref=dst, send_sem=send, recv_sem=recv, device_id=to, device_id_type=MESH).start()

    def split(kk):
        l = lax.div(kk, NC)
        c = lax.rem(kk, NC)
        return l, c, odd(c), lax.div(c, 2)

    def own_gu(kk):
        l, c, h, j = split(kk)
        wait_for(SGU.at[c], st_sem.at[kk])
        src, dst = SGU.at[c], wgu_f.at[l, c, :, pl.ds(pl.multiple_of(ROWS * s, ROWS), ROWS), :]
        for i in range(3):
            remote(src, dst, ags.at[kk], gi.at[kk], chip(i))
        remote(src, dst, ags.at[kk], gd.at[kk], partner)
        pltpu.make_async_copy(src, dst, gi.at[kk]).start()

    def forward_gu(kk):
        l, c, h, j = split(kk)
        wait_for(wgu_f.at[l, c, :, pl.ds(0, 256), :], gi.at[kk])
        for i in range(3):
            block = wgu_f.at[l, c, :, pl.ds(pl.multiple_of(ROWS * (2 * others[i] + e), ROWS), ROWS), :]
            remote(block, block, ags.at[kk], gd.at[kk], partner)

    def when_mine(kk, do):
        l, c, h, j = split(kk)

        @pl.when(h == e)
        def _():
            do(l, c, j)

    def own_d(kk):
        def do(l, c, j):
            src, dst = wd_h.at[l, pl.ds(pl.multiple_of(LANES * j + 32 * z, 32), 32), :], wd_f.at[l, c, q, z]
            for i in range(3):
                remote(src, dst, ads.at[kk], di.at[kk], chip(i))
            pltpu.make_async_copy(src, dst, di.at[kk]).start()
        when_mine(kk, do)

    def across_d(kk):
        def do(l, c, j):
            block = wd_f.at[l, c, :, z]
            wait_for(block, di.at[kk])
            for i in range(1, 4):
                remote(block, block, ads.at[kk], dz.at[kk], {"r": plane(i)})
        when_mine(kk, do)

    def forward_d(kk):
        def do(l, c, j):
            wait_for(wd_f.at[l, c, pl.ds(0, 3)], dz.at[kk])
            remote(wd_f.at[l, c], wd_f.at[l, c], ads.at[kk], dd.at[kk], partner)
        when_mine(kk, do)

    def arrive(kk):
        l, c, h, j = split(kk)
        wait_for(wgu_f.at[l, c, :, pl.ds(0, 256), :], gd.at[kk])

        @pl.when(h != e)
        def _():
            wait_for(wd_f.at[l, c], dd.at[kk])

    def stage(kk, _):
        l, c, h, j = split(kk)
        for p in range(4):
            cols = pl.ds(pl.multiple_of(384 * (2 * p + h) + LANES * j, LANES), LANES)
            for n, w in enumerate((wg_h, wu_h)):
                pltpu.make_async_copy(w.at[l, :, cols], SGU.at[c, n, :, pl.ds(LANES * p, LANES)], st_sem.at[kk]).start()
        return 0

    def gather_step(k):
        def go(do, kk):
            @pl.when(kk < NM)
            def _():
                do(kk)
        go(forward_gu, k)

        @pl.when(jnp.logical_and(k >= NC - 3, k + 3 < NM))
        def _():
            wait_for(wgu_f.at[0, 0, :, pl.ds(0, 448), :], ags.at[k + 3 - NC])
            stage(k + 3, 0)
        go(own_d, k + 3)
        go(own_gu, k + 2)
        go(across_d, k + 1)
        go(forward_d, k)

    def load(kk):
        l = lax.rem(lax.div(kk, NC), LAYERS)
        c, slot = lax.rem(kk, NC), odd(kk)
        pltpu.make_async_copy(wgu_f.at[l, c], WB.at[slot, pl.ds(0, 2)], wl_sem.at[slot]).start()
        for p in range(4):
            for y in range(Z):
                pltpu.make_async_copy(wd_f.at[l, c, p, y], WB.at[slot, 2, pl.ds(LANES * p + 32 * y, 32)], wl_sem.at[slot]).start()

    def loaded(kk):
        slot = odd(kk)
        wait_for(WB.at[slot], wl_sem.at[slot])

    def sent_all(kk):
        l, c, h, j = split(kk)
        @pl.when(kk >= NC)
        def _():
            wait_for(wgu_f.at[l, c, :, pl.ds(0, 448), :], ags.at[kk])

        @pl.when(h == e)
        def _():
            wait_for(wgu_f.at[l, c, :, pl.ds(0, 496), :], ads.at[kk])

    def place(m):
        l = 1 - lax.div(m, NC)
        c = lax.rem(m, NC)
        return l, c, odd(c), lax.div(c, 2), odd(m)

    def rows64(block):
        return pl.ds(pl.multiple_of(ROWS * block, ROWS), ROWS)

    def pair_send_gu(m, n):
        sl = odd(m)

        @pl.when(m >= 1)
        def _():
            wait_for(S1GU.at[n], rs.at[PAIR_OUT, n, 1 - sl])
        for p in range(4):
            S1GU[n, p] = DW[sl, n, rows64(2 * p + 1 - e), :].astype(bf16)
        remote(S1GU.at[n], R1GU.at[sl, n], rs.at[PAIR_OUT, n, sl], rs.at[PAIR_IN, n, sl], partner)

    def pair_send_d(m):
        l, c, h, j, sl = place(m)

        @pl.when(h != e)
        def _():
            @pl.when(m >= 2)
            def _():
                wait_for(S1D, rs.at[PAIR_OUT, DOWN, sl])
            for p in range(4):
                S1D[p] = DW[sl, 2, :, LANES * p:LANES * p + LANES].astype(bf16)
            remote(S1D, R1D, rs.at[PAIR_OUT, DOWN, sl], rs.at[PAIR_IN, DOWN, sl], partner)

    def pair_sum_gu(m, n):
        sl = odd(m)
        wait_for(R1GU.at[sl, n], rs.at[PAIR_IN, n, sl])

        @pl.when(m >= 1)
        def _():
            wait_for(R2GU.at[0, n], rs.at[PLANE_OUT, n, 1 - sl])
        for p in range(4):
            S2GU[n, p] = (DW[sl, n, rows64(2 * p + e), :] + R1GU[sl, n, p].astype(f32)).astype(bf16)
        P2GU[n] = DW[sl, n, rows64(2 * q + e), :] + R1GU[sl, n, q].astype(f32)
        for i in range(3):
            remote(S2GU.at[n, others[i]], R2GU.at[sl, n, i], rs.at[PLANE_OUT, n, sl], rs.at[PLANE_IN, n, sl], chip(i))

    def pair_sum_d(m):
        l, c, h, j, sl = place(m)

        @pl.when(h == e)
        def _():
            wait_for(R1D, rs.at[PAIR_IN, DOWN, sl])

            @pl.when(m >= 2)
            def _():
                wait_for(R2D, rs.at[PLANE_OUT, DOWN, sl])
            for p in range(4):
                total = DW[sl, 2, :, LANES * p:LANES * p + LANES] + R1D[p].astype(f32)
                S2D[p] = total.astype(bf16)

                @pl.when(q == p)
                def _():
                    P2D[...] = total
            for i in range(3):
                remote(S2D.at[others[i]], R2D.at[i], rs.at[PLANE_OUT, DOWN, sl], rs.at[PLANE_IN, DOWN, sl], chip(i))

    def ended_gu(m, n):
        wait_for(R3GU.at[0, n], rs.at[ROUND_IN, n, odd(m)])

    def ended_d(m):
        l, c, h, j, sl = place(m)

        @pl.when(h == e)
        def _():
            wait_for(R3D, rs.at[ROUND_IN, DOWN, sl])

    def plane_gu(m, n):
        sl = odd(m)
        wait_for(R2GU.at[sl, n], rs.at[PLANE_IN, n, sl])

        @pl.when(m >= 1)
        def _():
            wait_for(R3GU.at[0, n], rs.at[ACROSS_OUT, n, 1 - sl])

        @pl.when(m >= 2)
        def _():
            ended_gu(m - 2, n)
        for p in range(4):
            k = slice(QUARTER * p, QUARTER * p + QUARTER)
            total = P2GU[n, k, :]
            for i in range(3):
                total += R2GU[sl, n, i, k, :].astype(f32)
            S3GU[n, p] = total.astype(bf16)

            @pl.when(z == p)
            def _():
                P3GU[n] = total
        for i in range(1, 4):
            remote(S3GU.at[n, plane(i)], R3GU.at[sl, n, i - 1], rs.at[ACROSS_OUT, n, sl], rs.at[ACROSS_IN, n, sl], {"r": plane(i)})

    def plane_d(m):
        l, c, h, j, sl = place(m)

        @pl.when(h == e)
        def _():
            wait_for(R2D, rs.at[PLANE_IN, DOWN, sl])

            @pl.when(m >= 2)
            def _():
                wait_for(R3D, rs.at[ACROSS_OUT, DOWN, sl])
                ended_d(m - 2)
            for p in range(4):
                k = slice(LANES * p, LANES * p + LANES)
                total = P2D[k, :]
                for i in range(3):
                    total += R2D[i, k, :].astype(f32)
                S3D[p] = total.astype(bf16)

                @pl.when(z == p)
                def _():
                    P3D[...] = total
            for i in range(1, 4):
                remote(S3D.at[plane(i)], R3D.at[i - 1], rs.at[ACROSS_OUT, DOWN, sl], rs.at[ACROSS_IN, DOWN, sl], {"r": plane(i)})

    def last_gu(m, n):
        l, c, h, j, sl = place(m)
        wait_for(R3GU.at[sl, n], rs.at[ACROSS_IN, n, sl])

        @pl.when(m >= 1)
        def _():
            wait_for(S3GU.at[n], rs.at[ROUND_OUT, n, 1 - sl])
        S4GU[n] = (P3GU[n] + R3GU[sl, n, 0].astype(f32) + R3GU[sl, n, 1].astype(f32) + R3GU[sl, n, 2].astype(f32)).astype(bf16)
        dst = ogu_h.at[l, c, z, n]
        for i in range(1, 4):
            remote(S4GU.at[n], dst, rs.at[ROUND_OUT, n, sl], rs.at[ROUND_IN, n, sl], {"r": plane(i)})
        pltpu.make_async_copy(S4GU.at[n], dst, rs.at[ROUND_OUT, n, sl]).start()

    def last_d(m):
        l, c, h, j, sl = place(m)

        @pl.when(h == e)
        def _():
            wait_for(R3D, rs.at[ACROSS_IN, DOWN, sl])

            @pl.when(m >= 2)
            def _():
                wait_for(S3D, rs.at[ROUND_OUT, DOWN, sl])
            S4D[...] = (P3D[...] + R3D[0].astype(f32) + R3D[1].astype(f32) + R3D[2].astype(f32)).astype(bf16)
            dst = od_h.at[l, j, z]
            for i in range(1, 4):
                remote(S4D, dst, rs.at[ROUND_OUT, DOWN, sl], rs.at[ROUND_IN, DOWN, sl], {"r": plane(i)})
            pltpu.make_async_copy(S4D, dst, rs.at[ROUND_OUT, DOWN, sl]).start()

    def whole(gu, d, m):
        gu(m, 0)
        gu(m, 1)
        d(m)

    def pair_send(m):
        whole(pair_send_gu, pair_send_d, m)

    def pair_sum(m):
        whole(pair_sum_gu, pair_sum_d, m)

    def plane_sum(m):
        whole(plane_gu, plane_d, m)

    def last_sum(m):
        whole(last_gu, last_d, m)

    def first_half(kk):
        @pl.when(kk >= NC + 3)
        def _():
            last_sum(kk - NC - 3)

        @pl.when(kk >= NC + 1)
        def _():
            pair_send(kk - NC - 1)

    def second_half(kk):
        @pl.when(kk >= NC + 2)
        def _():
            plane_sum(kk - NC - 2)

        @pl.when(kk >= NC + 1)
        def _():
            pair_sum(kk - NC - 1)

    def tile(t, T):
        return pl.ds(pl.multiple_of(t * T, T), T)

    xin = pltpu.make_async_copy(x_h, HB, io_sem.at[0])
    dyin = pltpu.make_async_copy(dy_h, DY, io_sem.at[1])
    barrier = pltpu.get_barrier_semaphore()
    peers = [partner] + [chip(i) for i in range(3)] + [{"r": plane(i)} for i in range(1, 4)]
    for to in peers:
        pl.semaphore_signal(barrier, 1, device_id=to, device_id_type=MESH)
    stage(jnp.int32(0), 0)
    xin.start()
    dyin.start()
    lax.fori_loop(1, NC, stage, 0)
    pl.semaphore_wait(barrier, len(peers))
    own_d(jnp.int32(0))
    own_gu(jnp.int32(0))
    own_d(jnp.int32(1))
    own_d(jnp.int32(2))
    xin.wait()
    dyin.wait()

    def prepare(t, _):
        r = tile(t, TB)
        a = normed(HB[r, :])
        A[r, :] = a
        AT[:, r] = a.T
        DYT[:, r] = DY[r, :].T
        ACC[r, :] = jnp.zeros((TB, D), f32)
        return 0

    across_d(jnp.int32(0))
    lax.fori_loop(0, N // TB, prepare, 0)
    keep = pltpu.make_async_copy(AT, a0t_h, io_sem.at[2])
    keep.start()
    forward_gu(jnp.int32(0))
    own_gu(jnp.int32(1))
    own_d(jnp.int32(3))
    own_gu(jnp.int32(2))
    across_d(jnp.int32(1))
    forward_d(jnp.int32(0))
    arrive(jnp.int32(0))
    load(jnp.int32(0))

    NT = N // T // 2

    def rows_of(base, n, size=T):
        return pl.ds(pl.multiple_of(base + n, LANES), size)

    NT2 = N // T

    def saved(i):
        return gsave_h.at[lax.div(i, NT2), :, tile(lax.rem(i, NT2), T), :]

    def save(i, go):
        sl = odd(i)
        cp = pltpu.make_async_copy(GST.at[sl], saved(i), g_sem.at[sl])
        cp.start() if go else cp.wait()

    def phase0(i, _):
        kk, t, sl = lax.div(i, NT2), lax.rem(i, NT2), odd(i)

        @pl.when(t == 0)
        def _():
            loaded(kk)

        @pl.when(t == 1)
        def _():
            gather_step(kk + 1)

        @pl.when(t == NT2 - 1)
        def _():
            arrive(kk + 1)
            load(kk + 1)

        @pl.when(i >= 2)
        def _():
            save(i - 2, False)
        w = odd(kk)
        for b in range(T // SUB):
            rows, k = rows_of(t * T, SUB * b, SUB), slice(SUB * b, SUB * b + SUB)
            a = A[rows, :]
            g, u = nn(a, WB[w, 0]), nn(a, WB[w, 1])
            GST[sl, 0, k] = g
            GST[sl, 1, k] = u
            p = (g / (1.0 + jnp.exp(-g)) * u).astype(bf16)
            ACC[rows, :] += nn(p, WB[w, 2])
        save(i, True)
        return 0

    lax.fori_loop(0, NC * NT2, phase0, 0)
    keep.wait()

    def between(t, _):
        r = tile(t, TB)
        h = (HB[r, :].astype(f32) + ACC[r, :].astype(bf16).astype(f32)).astype(bf16)
        HB[r, :] = h
        a = normed(h)
        A[r, :] = a
        AT[:, r] = a.T
        ACC[r, :] = jnp.zeros((TB, D), f32)
        return 0

    lax.fori_loop(0, N // TB, between, 0)
    save(jnp.int32(NC * NT2 - 2), False)
    save(jnp.int32(NC * NT2 - 1), False)
    gather_step(jnp.int32(NC + 1))

    def backward(kk, base, n_tiles, first, g, u, ahead, late):
        w, sl, per = odd(kk), odd(kk), T // SUB
        done = {}

        def rows(k):
            return rows_of(base, SUB * k, SUB)

        def block(k):
            g_b, u_b = g(rows(k), k), u(rows(k), k)
            by_p = nt(DY[rows(k), :], WB[w, 2]).astype(bf16).astype(f32)
            sig = 1.0 / (1.0 + jnp.exp(-g_b))
            act = g_b * sig
            done[k] = ((by_p * u_b * (sig + act * (1.0 - sig))).astype(bf16), (by_p * act).astype(bf16), (act * u_b).astype(bf16))

        def by_data(k):
            if late:
                A[rows(k), :] = done[k][0]
                HB[rows(k), :] = done[k][1]
            else:
                ACC[rows(k), :] += nt(done[k][0], WB[w, 0]) + nt(done[k][1], WB[w, 1])

        def by_weights(tile_n):
            for m, left in ((2, DYT),) if late else ((2, DYT), (1, AT), (0, AT)):
                term = nn(left[:, rows_of(base, T * tile_n)], jnp.concatenate([done[per * tile_n + k][m] for k in range(per)]))
                DW[sl, m] = (jnp.where(first, 0.0, DW[sl, m]) if tile_n == 0 else DW[sl, m]) + term

        blocks = n_tiles * per
        for k in range(ahead):
            block(k)
        for k in range(blocks):
            if k + ahead < blocks:
                block(k + ahead)
            by_data(k)
            if (k + 1) % per == 0:
                by_weights(k // per)

    def phase1(i, _):
        kk, t = NC + lax.div(i, NT), lax.rem(i, NT)

        @pl.when(t == 0)
        def _():
            loaded(kk)
            first_half(kk)

        @pl.when(t == 1)
        def _():
            @pl.when(kk + 1 < NM)
            def _():
                arrive(kk + 1)
            load(kk + 1)
            gather_step(kk + 2)
            second_half(kk)
        w = odd(kk)
        backward(kk, t * (2 * T), 2, t == 0, lambda rows, b: nn(A[rows, :], WB[w, 0]), lambda rows, b: nn(A[rows, :], WB[w, 1]), 0, False)
        return 0

    lax.fori_loop(0, NC * NT, phase1, 0)
    again = pltpu.make_async_copy(a0t_h, AT, io_sem.at[2])
    again.start()

    def fetch(i, go):
        sl = odd(i)
        cp = pltpu.make_async_copy(saved(i), GST.at[sl], g_sem.at[sl])
        cp.start() if go else cp.wait()

    fetch(jnp.int32(0), True)

    def turn(t, _):
        r = tile(t, TB)
        by_a = ACC[r, :].astype(bf16).astype(f32)
        by_h = (DY[r, :].astype(f32) + through_norm(by_a, HB[r, :]).astype(bf16).astype(f32)).astype(bf16)
        DY[r, :] = by_h
        DYT[:, r] = by_h.T
        ACC[r, :] = jnp.zeros((TB, D), f32)
        return 0

    lax.fori_loop(0, N // TB, turn, 0)
    again.wait()

    def xtile(t, go):
        k = lax.rem(t, 3)
        cp = pltpu.make_async_copy(x_h.at[tile(t, TB)], WB.at[0, k], x_sem.at[k])
        cp.start() if go else cp.wait()

    end = jnp.int32(NM - 1)

    def backward_tile(i, late):
        kk, t, sl = 2 * NC + lax.div(i, NT2), lax.rem(i, NT2), odd(i)

        @pl.when(t == 0)
        def _():
            loaded(kk)
            first_half(kk)

        @pl.when(t == 1)
        def _():
            second_half(kk)

        if late:
            @pl.when(t == NT2 - 1)
            def _():
                last_gu(end - 2, 0)
                plane_gu(end - 1, 0)

        @pl.when(t == NT2 - 1)
        def _():
            if late:
                for k in range(3):
                    xtile(jnp.int32(k), True)
            else:
                load(kk + 1)

        @pl.when(i + 1 < NC * NT2)
        def _():
            fetch(i + 1, True)
        fetch(i, False)
        backward(kk, t * T, 1, t == 0, lambda rows, b: GST[sl, 0, SUB * b:SUB * b + SUB], lambda rows, b: GST[sl, 1, SUB * b:SUB * b + SUB], 1, late)
        return 0

    lax.fori_loop(0, (NC - 1) * NT2, lambda i, _: backward_tile(i, False), 0)
    lax.fori_loop((NC - 1) * NT2, NC * NT2, lambda i, _: backward_tile(i, True), 0)
    def finish(t, _):
        xtile(t, False)
        r = tile(t, TB)
        by_a = (ACC[r, :] + nt(A[r, :], WB[1, 0]) + nt(HB[r, :], WB[1, 1])).astype(bf16).astype(f32)
        DY[r, :] = (DY[r, :].astype(f32) + through_norm(by_a, WB[0, lax.rem(t, 3)]).astype(bf16).astype(f32)).astype(bf16)

        @pl.when(t + 3 < N // TB)
        def _():
            xtile(t + 3, True)
        return 0


    def finish_some(first, many):
        lax.fori_loop(first * N // TB // 8, (first + many) * N // TB // 8, finish, 0)

    pair_send_d(end)
    last_gu(end - 2, 1)
    last_d(end - 2)
    DW[1, 0] = nn(AT[...], A[...])
    pair_send_gu(end, 0)
    plane_gu(end - 1, 1)
    pair_sum_d(end)
    last_gu(end - 1, 0)
    DW[1, 1] = nn(AT[...], HB[...])
    pair_send_gu(end, 1)
    plane_d(end - 1)
    pair_sum_gu(end, 0)
    finish_some(0, 2)
    pair_sum_gu(end, 1)
    last_gu(end - 1, 1)
    finish_some(2, 2)
    plane_d(end)
    last_d(end - 1)
    finish_some(4, 1)
    plane_gu(end, 0)
    finish_some(5, 2)
    plane_gu(end, 1)
    last_d(end)
    finish_some(7, 1)
    last_gu(end, 0)
    pltpu.make_async_copy(DY, dx_h, io_sem.at[1]).start()
    last_gu(end, 1)

    def settle(kk, _):
        sent_all(kk)
        return 0

    lax.fori_loop(0, NM, settle, 0)
    for m in (end - 1, end):
        for n in range(2):
            ended_gu(m, n)
        ended_d(m)
    for n in range(2):
        wait_for(S1GU.at[n], rs.at[PAIR_OUT, n, 1])
        wait_for(R2GU.at[0, n], rs.at[PLANE_OUT, n, 1])
        wait_for(R3GU.at[0, n], rs.at[ACROSS_OUT, n, 1])
        wait_for(S3GU.at[n], rs.at[ROUND_OUT, n, 1])

    def sent_d(m):
        sl = m % 2
        wait_for(R2D, rs.at[PLANE_OUT, DOWN, sl])
        wait_for(R3D, rs.at[ACROSS_OUT, DOWN, sl])
        wait_for(S3D, rs.at[ROUND_OUT, DOWN, sl])

    @pl.when(e == 0)
    def _():
        wait_for(S1D, rs.at[PAIR_OUT, DOWN, 1])
        sent_d(NM - 2)

    @pl.when(e == 1)
    def _():
        wait_for(S1D, rs.at[PAIR_OUT, DOWN, 0])
        sent_d(NM - 1)
    wait_for(DY, io_sem.at[1])


def deliver(dx_i, gu_i, d_i, dx_o, g_o, u_o, d_o, DX, GU, DN, OG, OU, OD, sem_in, sem_out):
    parts = 4
    n = DX.shape[0] // parts
    moves = [(gu_i, GU), (d_i, DN)] + [(dx_i.at[pl.ds(n * i, n)], DX.at[pl.ds(n * i, n)]) for i in range(parts)]
    ins = [pltpu.make_async_copy(src, dst, sem_in.at[i]) for i, (src, dst) in enumerate(moves)]
    outs = [pltpu.make_async_copy(src, dst, sem_out.at[i]) for i, (src, dst) in enumerate(
        [(DX.at[pl.ds(n * i, n)], dx_o.at[pl.ds(n * i, n)]) for i in range(parts)] + [(OG, g_o), (OU, u_o), (OD, d_o)])]
    for cp in ins:
        cp.start()
    ins[0].wait()
    for l in range(LAYERS):
        for c in range(NC):
            for p in range(4):
                at = 384 * (2 * p + c % 2) + LANES * (c // 2)
                for y in range(Z):
                    OG[l, QUARTER * y:QUARTER * y + QUARTER, at:at + LANES] = GU[l, c, y, 0, :, LANES * p:LANES * p + LANES]
                    OU[l, QUARTER * y:QUARTER * y + QUARTER, at:at + LANES] = GU[l, c, y, 1, :, LANES * p:LANES * p + LANES]
    outs[parts].start()
    outs[parts + 1].start()
    ins[1].wait()
    for l in range(LAYERS):
        for j in range(3):
            for y in range(Z):
                OD[l, LANES * j:LANES * j + LANES, LANES * y:LANES * y + LANES] = DN[l, j, y].T
    outs[parts + 2].start()
    for i in range(parts):
        ins[2 + i].wait()
        outs[i].start()
    for cp in outs:
        cp.wait()


def solution(mesh, T=1024, TB=D):
    def step(x, dy, w_gate, w_up, w_down):
        N = x.shape[1]
        hbm = pl.BlockSpec(memory_space=pl.ANY)
        sds = jax.ShapeDtypeStruct
        v, dma = pltpu.VMEM, pltpu.SemaphoreType.DMA
        dx, ogu, od, *_ = pl.pallas_call(
            functools.partial(kernel, T, TB),
            name="step",
            out_shape=[
                sds((N, D), bf16), sds((LAYERS, NC, Z, 2, QUARTER, F), bf16), sds((LAYERS, 3, Z, LANES, LANES), bf16),
                sds((LAYERS, NC, 2, D, F), bf16), sds((LAYERS, NC, 4, Z, 32, D), bf16), sds((NC, 2, N, F), f32), sds((D, N), bf16),
            ],
            in_specs=[hbm] * 5,
            out_specs=[hbm] * 7,
            scratch_shapes=[
                v((N, D), bf16), v((D, N), bf16), v((N, D), bf16), v((D, N), bf16), v((N, D), bf16), v((N, D), f32),
                v((2, 3, D, D), bf16), v((2, 3, D, D), f32), v((2, 2, T, F), f32), v((NC, 2, ROWS, F), bf16),
                v((2, 4, ROWS, F), bf16), v((4, D, LANES), bf16), v((2, 2, 4, ROWS, F), bf16), v((4, D, LANES), bf16),
                v((2, 4, ROWS, F), bf16), v((4, D, LANES), bf16), v((2, ROWS, F), f32), v((D, LANES), f32), v((2, 2, 3, ROWS, F), bf16), v((3, D, LANES), bf16),
                v((2, 4, QUARTER, F), bf16), v((4, LANES, LANES), bf16), v((2, QUARTER, F), f32), v((LANES, LANES), f32), v((2, 2, 3, QUARTER, F), bf16), v((3, LANES, LANES), bf16),
                v((2, QUARTER, F), bf16), v((LANES, LANES), bf16),
                dma((NM,)), dma((3,)), dma((2,)), dma((2,)), *[dma((NM,)) for _ in range(7)], dma((3,)), dma((8, 3, 2)),
            ],
            compiler_params=pltpu.CompilerParams(collective_id=0, has_side_effects=True, vmem_limit_bytes=67043328),
        )(x[0], dy[0], w_gate, w_up, w_down)
        dx, *by_w = pl.pallas_call(
            deliver,
            name="deliver",
            out_shape=[sds((N, D), bf16), sds((LAYERS, ROWS, FF), bf16), sds((LAYERS, ROWS, FF), bf16), sds((LAYERS, 384, D), bf16)],
            in_specs=[hbm] * 3,
            out_specs=[hbm] * 4,
            scratch_shapes=[
                v((N, D), bf16), v((LAYERS, NC, Z, 2, QUARTER, F), bf16), v((LAYERS, 3, Z, LANES, LANES), bf16),
                v((LAYERS, ROWS, FF), bf16), v((LAYERS, ROWS, FF), bf16), v((LAYERS, 384, D), bf16), dma((6,)), dma((7,)),
            ],
            compiler_params=pltpu.CompilerParams(vmem_limit_bytes=67043328),
        )(dx, ogu, od)
        return dx[None], *by_w

    states, cut = P(("rep", "r", "s"), None, None), P(None, "s", None)
    return jax.shard_map(
        step,
        mesh=mesh,
        in_specs=(states, states) + (cut,) * 3,
        out_specs=(states,) + (P("rep", "s", None),) * 3,
        check_vma=False,
    )
```

time: 344 us -> 321 us (0.933)
  local copies, waits for them, and re-layouts: 13.5 us -> 0 us
  Pallas kernels: 329 us -> 320 us
    pallas_call x1 -> x2, Pallas kernels: 329 us -> 320 us  [the longest x1 315 us: step(): pl.pallas_call(functools.partial(kernel, T, TB), name='step', out_shape=[...]
    unnamed x3 -> x0, local copies, waits for them, and re-layouts: 4.47 us -> none
    reshape x3 -> x0, local copies, waits for them, and re-layouts: 3.75 us -> none  [the longest x2 2.57 us: step(): ogu.reshape(LAYERS, 3, 2, Z, 2, 16, 4, 128)]
where the time goes in v2:
time: 321 us; the launch traced here: 320 us
  Pallas kernels  320 us (100%)
    pallas_call x1, Pallas kernels, step(): pl.pallas_call(functools.partial(kernel, T, TB), name='step', out_shape=[...  315 us

profile of v2, /device:TPU:0, one launch (start us, length us, event | category | flops | bytes accessed | tf_op | source)
XLA Modules:
  0.0 320.4 jit_solution(17140085122194990194)
XLA Ops:
  0.6 315.0 %step.1 = (bf16[4096,512]{1,0:T(8,128)(2,1)}, bf16[2,6,4,2,16,512]{5,4,3,2,1,0:T(8,128)(2,1)}, bf16[2,3,4,128,128]{4,3,2,1,0:T(8,128)(2,1)}, bf16[2,6,2,512,512]...) custom-call(bf16[4096,512]{1,0:T(8,128)(2,1)} %bitcast.3, ...), custom_call_target="tpu_custom_call" | custom-call | tf_op jit(solution)/shard_map/step/pallas_call | solution.py:701
  315.7 4.6 %deliver.1 = (bf16[4096,512]{1,0:T(8,128)(2,1)}, bf16[2,64,3072]{2,1,0:T(8,128)(2,1)}, bf16[2,64,3072]{2,1,0:T(8,128)(2,1)}, bf16[2,384,512]{2,1,0:T(8,128)(2,1)}) custom-call(bf16[4096,512]{1,0:T(8,128)(2,1)} %get-tuple-element.11.dx_i, bf16[2,6,4,2,16,512]{5,4,3,2,1,0:T(8,128)(2,1)} %get-tuple-element.12.gu_i, ...), custom_call_target="tpu_custom_call" | custom-call | tf_op jit(solution)/shard_map/deliver/pallas_call | solution.py:721
